TPU v7x, 32 devices: a whole 2x2x4 slice. The times are simulated.
32 devices in a mesh: freq: 8 (over z, core), tm: 4 (over y, x).
Axes of the slice: x: 2, y: 2, z: 4, core: 2. Of those that a mesh axis runs over, the one named last changes fastest.
Arguments:
- band_state: float32 [2048, 4096], P('freq', 'tm'), may hold values from -2.5 to 2.5
- lower_rows: int32 [3, 2048], replicated, may hold values from 0 to 2047, as said below
- upper_rows: int32 [3, 2048], replicated, may hold values from 0 to 2047, as said below
- delays: int32 [3, 2048], replicated, may hold values from 0 to 1024, as said below
- counts: int32 [7], replicated, may hold values from 256 to 2048, as said below
Outputs:
- dedispersed: float32 [2048, 4096], P('freq', 'tm')
Inputs may be any that keep to these rules, and one draw needn't show every extreme that they name: `counts`: entry 8 - 8 / 2^k + b is the live row count of output sub-band b of iteration k; it lies between half and all of that sub-band's 2 * 2048 / 2^(3 - k) padded rows, and in every iteration some sub-band has all its rows live. With w = 2048 / 2^(3 - k), lower_rows[k, i] is a row of input sub-band 2 * floor(i / (2 * w)) whose position in that sub-band is below its live count (all w rows are live in iteration 0). With w = 2048 / 2^(3 - k), upper_rows[k, i] is a row of input sub-band 2 * floor(i / (2 * w)) + 1 whose position in that sub-band is below its live count (all w rows are live in iteration 0). delays[k, i] is at most 2048 / 2^(3 - k), and equals it at some row in every iteration.
All inputs are finite; a program needn't handle non-finite values.
Results may differ from a plain program's by a relative error of at most 0.0003.
Values sent between devices are 32-bit elements; how exact they have to be, the bound alone decides.
A program may use at most 64 MiB of HBM per device.

v0:
```python
import jax
import jax.numpy as jnp
from jax import lax
from jax.sharding import PartitionSpec as P

DMAX = 2048
ITERS = 3


def shifted_2(block, axis, distance):
    devices = range(lax.axis_size(axis))
    route = [(i - distance, i) for i in devices if i - distance in devices]
    return lax.ppermute(block, axis, route)


def delay_columns(extended, shifts, widest):
    row_count = extended.shape[0]
    for bit_index in range(widest.bit_length()):
        stride = 1 << bit_index
        shifted = jnp.concatenate(
            [jnp.zeros((row_count, stride), extended.dtype), extended[:, :-stride]], axis=1
        )
        extended = jnp.where((shifts >> bit_index & 1)[:, None] == 1, shifted, extended)
    return extended


def live_mask(global_rows, counts, width_out, offset, bands_out):
    band_index = global_rows // width_out
    band_counts = counts[offset : offset + bands_out]
    matches = band_index[:, None] == jnp.arange(bands_out, dtype=jnp.int32)[None, :]
    live_count = jnp.sum(jnp.where(matches, band_counts[None, :], 0), axis=1)
    return global_rows % width_out < live_count


def per_device(band_state, lower_rows, upper_rows, delays, counts):
    row_count, samples = band_state.shape
    freq_index = lax.axis_index("freq")
    first_row = freq_index * row_count
    global_rows = first_row + jnp.arange(row_count, dtype=jnp.int32)
    current = band_state
    for iteration in range(ITERS):
        width_in = DMAX >> ITERS - iteration
        width_out = 2 * width_in
        bands_out = DMAX // width_out
        offset = 2**ITERS - 2 ** (ITERS - iteration)
        lower_source = lax.dynamic_slice_in_dim(lower_rows[iteration], first_row, row_count)
        upper_source = lax.dynamic_slice_in_dim(upper_rows[iteration], first_row, row_count)
        own_delays = lax.dynamic_slice_in_dim(delays[iteration], first_row, row_count)
        gathered = lax.all_gather(current, "freq", axis=0, tiled=True)
        lower_values = jnp.take(gathered, lower_source, axis=0)
        upper_values = jnp.take(gathered, upper_source, axis=0)
        rim_columns = shifted_2(upper_values[:, samples - width_in :], "tm", 1)
        extended = jnp.concatenate([rim_columns, upper_values], axis=1)
        delayed = delay_columns(extended, own_delays, width_in)[:, width_in:]
        live_rows = live_mask(global_rows, counts, width_out, offset, bands_out)
        current = jnp.where(live_rows[:, None], lower_values + delayed, jnp.zeros_like(delayed))
    return current


def solution(mesh):
    return jax.shard_map(
        per_device,
        mesh=mesh,
        in_specs=(P("freq", "tm"), P(), P(), P(), P()),
        out_specs=P("freq", "tm"),
        check_vma=False,
    )
```

profile of v0, /device:TPU:7, one launch (start us, length us, event | category | flops | bytes accessed | tf_op | source)
XLA Modules:
  0.0 347.8 jit_solution(9411557968534590565)
XLA Ops:
  6.5 0.7 all-gather.4.cloned.1.call-update
  7.3 0.9 fusion.17
  8.2 0.9 fusion.19
  9.2 0.7 select_reduce_fusion
  9.9 0.9 fusion.18
  10.8 81.7 %all-gather.4.cloned.1.call-done = f32[2048,1024]{1,0:T(8,128)} async-done(((f32[256,1024]{1,0:T(8,128)}), f32[2048,1024]{1,0:T(8,128)}) %all-gather.4.cloned.1.call-update) | async-done | bytes 8388624 | tf_op jit(solution)/shard_map/all_gather | solution.py:49
  92.6 4.9 %gather_fusion.1 = f32[256,1024]{1,0:T(8,128)S(1)} fusion(f32[2048,1024]{1,0:T(8,128)} %all-gather.4.cloned.1.call-done, s32[1024]{0:T(1024)S(1)} %pad_clamp_fusion.4), kind=kCustom, calls=%fused_computation.1.clone | custom fusion | bytes 2098176 | tf_op jit(solution)/shard_map/jit(_take)/gather | solution.py:51
  97.5 0.1 broadcast_select_fusion.2
  97.7 1.3 collective-permute-start
  99.1 4.9 %gather_fusion = f32[256,1024]{1,0:T(8,128)S(1)} fusion(f32[2048,1024]{1,0:T(8,128)} %all-gather.4.cloned.1.call-done, s32[1024]{0:T(1024)S(1)} %pad_clamp_fusion.5), kind=kCustom, calls=%fused_computation.clone | custom fusion | bytes 2098176 | tf_op jit(solution)/shard_map/jit(_take)/gather | solution.py:50
  104.1 3.1 collective-permute-done
  107.2 0.1 fusion.4
  107.3 0.5 fusion.5
  107.8 0.5 pad_select_fusion.23
  108.2 0.5 pad_select_fusion.22
  108.7 0.5 pad_select_fusion.21
  109.2 0.5 pad_select_fusion.20
  109.7 0.5 pad_select_fusion.19
  110.2 0.5 pad_select_fusion.18
  110.7 0.2 pad_select_fusion.17
  110.9 0.1 slice.210
  111.1 1.2 fusion.11
  112.7 81.2 %all-gather.6.cloned.1.call-done = f32[2048,1024]{1,0:T(8,128)} async-done(((f32[256,1024]{1,0:T(8,128)}), f32[2048,1024]{1,0:T(8,128)}) %all-gather.6.cloned.1.call-update) | async-done | bytes 8388624 | tf_op jit(solution)/shard_map/all_gather | solution.py:49
  193.9 4.9 %gather_fusion.3 = f32[256,1024]{1,0:T(8,128)S(1)} fusion(f32[2048,1024]{1,0:T(8,128)} %all-gather.6.cloned.1.call-done, s32[1024]{0:T(1024)S(1)} %pad_clamp_fusion.2), kind=kCustom, calls=%fused_computation.3.clone | custom fusion | bytes 2098176 | tf_op jit(solution)/shard_map/jit(_take)/gather | solution.py:51
  198.8 0.1 broadcast_select_fusion.1
  199.0 1.5 collective-permute-start.1
  200.5 4.9 %gather_fusion.2 = f32[256,1024]{1,0:T(8,128)S(1)} fusion(f32[2048,1024]{1,0:T(8,128)} %all-gather.6.cloned.1.call-done, s32[1024]{0:T(1024)S(1)} %pad_clamp_fusion.3), kind=kCustom, calls=%fused_computation.2.clone | custom fusion | bytes 2098176 | tf_op jit(solution)/shard_map/jit(_take)/gather | solution.py:50
  205.5 8.6 %collective-permute-done.1 = f32[256,512]{1,0:T(8,128)S(1)} collective-permute-done((f32[256,512]{1,0:T(8,128)S(1)}, f32[256,512]{1,0:T(8,128)S(1)}, u32[]{:S(2)}, u32[]{:S(2)}) %collective-permute-start.1) | collective-permute-done | bytes 524320 | tf_op jit(solution)/shard_map/ppermute | solution.py:13
  214.1 0.1 fusion.2
  214.2 0.6 fusion.3
  214.8 0.6 pad_select_fusion.16
  215.4 0.6 pad_select_fusion.15
  215.9 0.6 pad_select_fusion.14
  216.5 0.6 pad_select_fusion.13
  217.1 0.6 pad_select_fusion.12
  217.7 0.6 pad_select_fusion.11
  218.3 0.1 slice.221
  218.4 0.2 pad_select_fusion.10
  218.6 0.1 slice.222
  218.7 0.2 pad_select_fusion.9
  219.0 1.2 fusion.9
  220.3 81.5 %all-gather.8.cloned.1.call-done = f32[2048,1024]{1,0:T(8,128)} async-done(((f32[256,1024]{1,0:T(8,128)}), f32[2048,1024]{1,0:T(8,128)}) %all-gather.8.cloned.1.call-update) | async-done | bytes 8388624 | tf_op jit(solution)/shard_map/all_gather | solution.py:49
  301.8 4.9 %gather_fusion.5 = f32[256,1024]{1,0:T(8,128)S(1)} fusion(f32[2048,1024]{1,0:T(8,128)} %all-gather.8.cloned.1.call-done, s32[1024]{0:T(1024)S(1)} %pad_clamp_fusion), kind=kCustom, calls=%fused_computation.5.clone | custom fusion | bytes 2098176 | tf_op jit(solution)/shard_map/jit(_take)/gather | solution.py:51
  306.7 0.1 broadcast_select_fusion
  306.9 1.5 collective-permute-start.2
  308.4 0.6 slice.141
  309.0 0.7 fusion.13
  309.7 4.9 %gather_fusion.4 = f32[256,1024]{1,0:T(8,128)S(1)} fusion(f32[2048,1024]{1,0:T(8,128)} %all-gather.8.cloned.1.call-done, s32[1024]{0:T(1024)S(1)} %pad_clamp_fusion.1), kind=kCustom, calls=%fused_computation.4.clone | custom fusion | bytes 2098176 | tf_op jit(solution)/shard_map/jit(_take)/gather | solution.py:50
  314.7 18.5 %collective-permute-done.2 = f32[256,1024]{1,0:T(8,128)S(1)} collective-permute-done((f32[256,1024]{1,0:T(8,128)S(1)}, f32[256,1024]{1,0:T(8,128)S(1)}, u32[]{:S(2)}, u32[]{:S(2)}) %collective-permute-start.2) | collective-permute-done | bytes 1048608 | tf_op jit(solution)/shard_map/ppermute | solution.py:13
  333.2 0.1 fusion
  333.4 0.7 fusion.1
  334.1 0.7 pad_select_fusion.8
  334.9 0.7 pad_select_fusion.7
  335.6 0.7 pad_select_fusion.6
  336.4 0.7 pad_select_fusion.5
  337.1 0.7 pad_select_fusion.4
  337.9 0.7 pad_select_fusion.3
  338.6 0.2 slice.233
  338.8 0.3 pad_select_fusion.2
  339.1 0.1 slice.234
  339.2 0.3 pad_select_fusion.1
  339.5 0.1 slice.235
  339.6 0.2 pad_select_fusion
  340.0 1.3 fusion.7
  (41 shorter events, 0.9 us)
Async XLA Ops:
  6.5 86.0 %all-gather.4.cloned.1.call-start = ((), (), s32[]{:S(2)}) async-start(), calls=%async_computation | async-start | bytes 9437184 | tf_op jit(solution)/shard_map/all_gather | solution.py:49
  7.3 186.6 %all-gather.6.cloned.1.call-start = ((), (), s32[]{:S(2)}) async-start(), calls=%async_computation.1 | async-start | bytes 9437184 | tf_op jit(solution)/shard_map/all_gather | solution.py:49
  97.7 9.5 %collective-permute-start = (f32[256,256]{1,0:T(8,128)S(1)}, f32[256,256]{1,0:T(8,128)S(1)}, u32[]{:S(2)}, u32[]{:S(2)}) collective-permute-start(f32[256,256]{1,0:T(8,128)S(1)} %slice.200), channel_id=1, source_target_pairs={{0,1},{1,2},{2,3},{4,5},{5,6},{6,7},{8,9},{9,10},{10,11},{12,13},{... | collective-permute-start | bytes 786440 | tf_op jit(solution)/shard_map/ppermute | solution.py:13
  111.1 1.3 copy-start
  112.3 189.5 %all-gather.8.cloned.1.call-start = ((), (), s32[]{:S(2)}) async-start(), calls=%async_computation.2 | async-start | bytes 9437184 | tf_op jit(solution)/shard_map/all_gather | solution.py:49
  199.0 15.1 %collective-permute-start.1 = (f32[256,512]{1,0:T(8,128)S(1)}, f32[256,512]{1,0:T(8,128)S(1)}, u32[]{:S(2)}, u32[]{:S(2)}) collective-permute-start(f32[256,512]{1,0:T(8,128)S(1)} %slice.212), channel_id=1, source_target_pairs={{0,1},{1,2},{2,3},{4,5},{5,6},{6,7},{8,9},{9,10},{10,11},{12,13},{... | collective-permute-start | bytes 1572872 | tf_op jit(solution)/shard_map/ppermute | solution.py:13
  306.9 26.3 %collective-permute-start.2 = (f32[256,1024]{1,0:T(8,128)S(1)}, f32[256,1024]{1,0:T(8,128)S(1)}, u32[]{:S(2)}, u32[]{:S(2)}) collective-permute-start(f32[256,1024]{1,0:T(8,128)S(1)} %broadcast_select_fusion), channel_id=1, source_target_pairs={{0,1},{1,2},{2,3},{4,5},{5,6},{6,7},{8,9},{9,10},{10,11},{12,13},{... | collective-permute-start | bytes 3145736 | tf_op jit(solution)/shard_map/ppermute | solution.py:13
Sparse Core Ops, SparseCore 0:
  8.9 83.6 all-gather.3
  112.4 81.3 all-gather.5
  220.4 81.3 all-gather.7
where the time goes:
time: 350 us; the launch traced here: 348 us
  waiting for transfers between devices  275 us (79%)
  local copies, waits for them, and re-layouts  34.1 us (10%)
  other arithmetic  20.2 us (6%)
  between operations  13.7 us (4%)
  starting transfers between devices  4.36 us (1%)
    all_gather x3, waiting for transfers between devices, per_device(): gathered = lax.all_gather(current, 'freq', axis=0, tiled=True)  244 us
    ppermute x3, waiting for transfers between devices, shifted_2(): return lax.ppermute(block, axis, route)  30.3 us
    gather x3, local copies, waits for them, and re-layouts, per_device(): lower_values = jnp.take(gathered, lower_source, axis=0)  14.8 us
    gather x3, local copies, waits for them, and re-layouts, per_device(): upper_values = jnp.take(gathered, upper_source, axis=0)  14.8 us
    select_n x27, other arithmetic, delay_columns(): jnp.where((shifts >> bit_index & 1)[:, None] == 1, shifted, extended)  13.9 us
  transfers between devices with their start and end apart: 6, of which 6 were waited for; matrix products, arithmetic and copies ran while one was open for 6% of the time, Pallas kernels for 0%

commit v1 on v0

--- a/solution.py
+++ b/solution.py
@@ -1,10 +1,18 @@
+import functools
+
 import jax
 import jax.numpy as jnp
 from jax import lax
+from jax.experimental import pallas as pl
+from jax.experimental.pallas import tpu as pltpu
 from jax.sharding import PartitionSpec as P
 
 DMAX = 2048
 ITERS = 3
+LANES = 128
+UNROLL = 8
+CHUNKS_1 = 8
+CHUNKS_2 = 16
 
 
 def shifted_2(block, axis, distance):
@@ -32,7 +40,7 @@
     return global_rows % width_out < live_count
 
 
-def per_device(band_state, lower_rows, upper_rows, delays, counts):
+def per_device_general(band_state, lower_rows, upper_rows, delays, counts):
     row_count, samples = band_state.shape
     freq_index = lax.axis_index("freq")
     first_row = freq_index * row_count
@@ -57,9 +65,261 @@
     return current
 
 
+class Flow:
+    def __init__(self, buffer, sems, first, chunk):
+        self.buffer, self.sems, self.first, self.chunk = buffer, sems, first, chunk
+
+    def copy(self, j, row, target, source_at, target_at, size):
+        rows = pl.ds(row + j * self.chunk, self.chunk)
+        return pltpu.make_async_remote_copy(
+            src_ref=self.buffer.at[rows, pl.ds(source_at, size)],
+            dst_ref=self.buffer.at[rows, pl.ds(target_at, size)],
+            send_sem=self.sems.at[0, self.first + j],
+            recv_sem=self.sems.at[1, self.first + j],
+            device_id=target,
+            device_id_type=pl.DeviceIdType.MESH,
+        )
+
+
+def kernel(tiles, tm_size, x_ref, lower, upper, delays, counts, out_ref, b0, b1, b2, s0, s1, s2, local_sem):
+    f, t = lax.axis_index("freq"), lax.axis_index("tm")
+    c, z = lax.rem(f, 2), lax.div(f, 2)
+    zb, half = lax.rem(z, 2), lax.div(z, 2)
+    z_size = 2 ** (ITERS - 1)
+    rows = x_ref.shape[0]
+    at = lambda ff, tt: {"freq": ff, "tm": tt}
+    partner = at(f + 1 - 2 * c, t)
+    later = at(f, t + 1)
+    pair = at(f + 2 - 4 * zb, t)
+    inner = zb != half
+    facing = at(f + 2 - 4 * half, t)
+    outer = at(f - 2 + 4 * half, t)
+    has_later, has_earlier = t < tm_size - 1, t > 0
+
+    barrier = pltpu.get_barrier_semaphore()
+
+    def greet(target):
+        pl.semaphore_signal(barrier, inc=1, device_id=target, device_id_type=pl.DeviceIdType.MESH)
+
+    greet(partner)
+    for cond, target in (
+        (z > 0, at(f - 2, t)),
+        (z < z_size - 1, at(f + 2, t)),
+        (has_earlier, at(f, t - 1)),
+        (has_later, later),
+    ):
+        pl.when(cond)(functools.partial(greet, target))
+    one = lambda cond: jnp.where(cond, 1, 0)
+    pl.semaphore_wait(barrier, 1 + one(z > 0) + one(z < z_size - 1) + one(has_earlier) + one(has_later))
+
+    lane = lax.broadcasted_iota(jnp.int32, (tiles, LANES), 1)
+
+    def merge(k, source, first, position, start, count, store):
+        width_in = DMAX >> ITERS - k
+        rim = width_in // LANES
+        width_out = 2 * width_in
+        band = lax.div(first, width_out)
+        limit = counts[2**ITERS - 2 ** (ITERS - k) + band]
+        wrap = width_out - 1
+
+        def body(step, carry):
+            values = []
+            for u in range(UNROLL):
+                i = start + step * UNROLL + u
+                g = first + i
+                lo, up, d = lower[k, g] & wrap, upper[k, g] & wrap, delays[k, g]
+                q, r = d >> 7, d & (LANES - 1)
+                a = source[up, pl.ds(tiles - q, tiles), :]
+                b = source[up, pl.ds(jnp.maximum(tiles - 1 - q, tiles - rim), tiles), :]
+                a, b = pltpu.roll(a, r, 1), pltpu.roll(b, r, 1)
+                total = source[lo, tiles:, :] + jnp.where(lane >= r, a, b)
+                values.append((i, jnp.where(position + i < limit, total, jnp.zeros_like(total))))
+            for i, value in values:
+                store(i, value)
+            return carry
+
+        lax.fori_loop(0, count // UNROLL, body, 0)
+
+    def when(cond, action):
+        pl.when(cond)(action)
+
+    rim0 = rows // LANES
+    own0 = Flow(b0, s0, 0, rows)
+    rim_out0 = Flow(b0, s0, 1, rows)
+    rim_in0 = Flow(b0, s0, 2, rows)
+    stage = pltpu.make_async_copy(x_ref, b0.at[pl.ds(c * rows, rows), pl.ds(tiles, tiles)], local_sem.at[0])
+    stage.start()
+    stage.wait()
+    own0.copy(0, c * rows, partner, tiles, tiles, tiles).start()
+    upper0 = rows
+    send_rim0 = rim_out0.copy(0, upper0, later, 2 * tiles - rim0, tiles - rim0, rim0)
+    pass_rim0 = rim_in0.copy(0, upper0, partner, tiles - rim0, tiles - rim0, rim0)
+    when((c == 1) & has_later, send_rim0.start)
+
+    @pl.when(t == 0)
+    def _():
+        for buffer in (b0, b1, b2):
+            first = buffer.shape[0] // 2
+
+            def clear(i, carry, buffer=buffer, first=first):
+                for u in range(UNROLL):
+                    buffer[first + i * UNROLL + u, :tiles, :] = jnp.zeros((tiles, LANES), jnp.float32)
+                return carry
+
+            lax.fori_loop(0, first // UNROLL, clear, 0)
+
+    @pl.when((c == 1) & has_earlier)
+    def _():
+        send_rim0.wait_recv()
+        pass_rim0.start()
+
+    own0.copy(0, (1 - c) * rows, partner, tiles, tiles, tiles).wait_recv()
+    when((c == 0) & has_earlier, pass_rim0.wait_recv)
+
+    rim1 = 2 * rows // LANES
+    n1, chunk1 = CHUNKS_1, rows // CHUNKS_1
+    flows1 = [Flow(b1, s1, kind * n1, chunk1) for kind in range(5)]
+    own1, pair1, pass1, rim_out1, rim_in1 = flows1
+    mine1 = zb * 2 * rows + c * rows
+    other1 = (1 - zb) * 2 * rows + c * rows
+    upper1 = 2 * rows + c * rows
+    wide = (tiles, tiles, tiles)
+    tail1 = (2 * tiles - rim1, tiles - rim1, rim1)
+    kept1 = (tiles - rim1, tiles - rim1, rim1)
+
+    def store1(i, value):
+        b1[mine1 + i, tiles:, :] = value
+
+    for j in range(n1):
+        merge(0, b0, f * rows, c * rows, j * chunk1, chunk1, store1)
+        pair1.copy(j, mine1, pair, *wide).start()
+        own1.copy(j, mine1, partner, *wide).start()
+        when((zb == 1) & has_later, rim_out1.copy(j, upper1, later, *tail1).start)
+    for j in range(n1):
+        pair1.copy(j, other1, pair, *wide).wait_recv()
+        when((zb == 0) & has_later, rim_out1.copy(j, upper1, later, *tail1).start)
+        pass1.copy(j, other1, partner, *wide).start()
+
+        @pl.when(has_earlier)
+        def _():
+            rim_out1.copy(j, upper1, later, *tail1).wait_recv()
+            rim_in1.copy(j, upper1, partner, *kept1).start()
+
+    across = (1 - 2 * c) * rows
+    for j in range(n1):
+        own1.copy(j, mine1 + across, partner, *wide).wait_recv()
+        pass1.copy(j, other1 + across, partner, *wide).wait_recv()
+        when(has_earlier, rim_in1.copy(j, upper1 + across, partner, *kept1).wait_recv)
+
+    n2, chunk2 = CHUNKS_2, 2 * rows // CHUNKS_2
+    flows2 = [Flow(b2, s2, kind * n2, chunk2) for kind in range(5)]
+    own2, z2, pass2, rim_out2, rim_in2 = flows2
+    mine2 = half * 4 * rows + c * 2 * rows
+    other2 = (1 - half) * 4 * rows + c * 2 * rows
+    upper2 = 4 * rows + c * 2 * rows
+    tail2 = (tiles, 0, tiles)
+    kept2 = (0, 0, tiles)
+
+    def store2(i, value):
+        b2[mine2 + i, tiles:, :] = value
+
+    for j in range(n2):
+        merge(1, b1, half * 4 * rows + c * 2 * rows, c * 2 * rows, j * chunk2, chunk2, store2)
+        when(inner, z2.copy(j, mine2, facing, *wide).start)
+        when((half == 1) & has_later, rim_out2.copy(j, upper2, later, *tail2).start)
+        own2.copy(j, mine2, partner, *wide).start()
+    for j in range(n2):
+        z2.copy(j, other2, partner, *wide).wait_recv()
+        when(
+            inner,
+            pltpu.make_async_remote_copy(
+                src_ref=b2.at[pl.ds(other2 + j * chunk2, chunk2), pl.ds(tiles, tiles)],
+                dst_ref=b2.at[pl.ds(other2 + j * chunk2, chunk2), pl.ds(tiles, tiles)],
+                send_sem=s2.at[0, 5 * n2 + j],
+                recv_sem=s2.at[1, n2 + j],
+                device_id=outer,
+                device_id_type=pl.DeviceIdType.MESH,
+            ).start,
+        )
+        when((half == 0) & has_later, rim_out2.copy(j, upper2, later, *tail2).start)
+        pass2.copy(j, other2, partner, *wide).start()
+
+        @pl.when(has_earlier)
+        def _():
+            rim_out2.copy(j, upper2, later, *tail2).wait_recv()
+            rim_in2.copy(j, upper2, partner, *kept2).start()
+
+    across = (1 - 2 * c) * 2 * rows
+    for j in range(n2):
+        own2.copy(j, mine2 + across, partner, *wide).wait_recv()
+        pass2.copy(j, other2 + across, partner, *wide).wait_recv()
+        when(has_earlier, rim_in2.copy(j, upper2 + across, partner, *kept2).wait_recv)
+
+    def store_out(i, value):
+        out_ref[i] = value
+
+    merge(2, b2, f * rows, f * rows, 0, rows, store_out)
+
+    own0.copy(0, c * rows, partner, *wide).wait_send()
+    when((c == 1) & has_later, send_rim0.wait_send)
+    when((c == 1) & has_earlier, pass_rim0.wait_send)
+    for j in range(n1):
+        pair1.copy(j, mine1, pair, *wide).wait_send()
+        own1.copy(j, mine1, partner, *wide).wait_send()
+        pass1.copy(j, other1, partner, *wide).wait_send()
+        when(has_later, rim_out1.copy(j, upper1, later, *tail1).wait_send)
+        when(has_earlier, rim_in1.copy(j, upper1, partner, *kept1).wait_send)
+    for j in range(n2):
+        own2.copy(j, mine2, partner, *wide).wait_send()
+        pass2.copy(j, other2, partner, *wide).wait_send()
+        when(has_later, rim_out2.copy(j, upper2, later, *tail2).wait_send)
+        when(has_earlier, rim_in2.copy(j, upper2, partner, *kept2).wait_send)
+
+        @pl.when(inner)
+        def _():
+            z2.copy(j, mine2, facing, *wide).wait_send()
+            pltpu.make_async_remote_copy(
+                src_ref=b2.at[pl.ds(other2 + j * chunk2, chunk2), pl.ds(tiles, tiles)],
+                dst_ref=b2.at[pl.ds(other2 + j * chunk2, chunk2), pl.ds(tiles, tiles)],
+                send_sem=s2.at[0, 5 * n2 + j],
+                recv_sem=s2.at[1, n2 + j],
+                device_id=outer,
+                device_id_type=pl.DeviceIdType.MESH,
+            ).wait_send()
+
+
+def per_device_fused(tm_size, band_state, lower_rows, upper_rows, delays, counts):
+    row_count, samples = band_state.shape
+    tiles = samples // LANES
+    dma = pltpu.SemaphoreType.DMA
+    out = pl.pallas_call(
+        functools.partial(kernel, tiles, tm_size),
+        out_shape=jax.ShapeDtypeStruct((row_count, tiles, LANES), jnp.float32),
+        in_specs=[pl.BlockSpec(memory_space=pltpu.VMEM)] + [pl.BlockSpec(memory_space=pltpu.SMEM)] * 4,
+        out_specs=pl.BlockSpec(memory_space=pltpu.VMEM),
+        scratch_shapes=[
+            pltpu.VMEM((2 * row_count, 2 * tiles, LANES), jnp.float32),
+            pltpu.VMEM((4 * row_count, 2 * tiles, LANES), jnp.float32),
+            pltpu.VMEM((8 * row_count, 2 * tiles, LANES), jnp.float32),
+            dma((2, 3)),
+            dma((2, 5 * CHUNKS_1)),
+            dma((2, 6 * CHUNKS_2)),
+            dma((1,)),
+        ],
+        compiler_params=pltpu.CompilerParams(
+            collective_id=0, has_side_effects=True, vmem_limit_bytes=60 * 2**20
+        ),
+    )(band_state.reshape(row_count, tiles, LANES), lower_rows, upper_rows, delays, counts)
+    return out.reshape(row_count, samples)
+
+
 def solution(mesh):
+    if mesh.shape["freq"] == 2**ITERS:
+        body = functools.partial(per_device_fused, mesh.shape["tm"])
+    else:
+        body = per_device_general
     return jax.shard_map(
-        per_device,
+        body,
         mesh=mesh,
         in_specs=(P("freq", "tm"), P(), P(), P(), P()),
         out_specs=P("freq", "tm"),

time: 350 us -> 109 us (0.31)
  waiting for transfers between devices: 275 us -> 0 us
  Pallas kernels: 0 us -> 104 us
  local copies, waits for them, and re-layouts: 34.1 us -> 4.78 us
  other arithmetic: 20.2 us -> 0 us
  between operations: 13.7 us -> 0.01 us
  starting transfers between devices: 4.36 us -> 0 us
    all_gather x3 -> x0, waiting for transfers between devices: 244 us -> none  [per_device(): gathered = lax.all_gather(current, 'freq', axis=0, tiled=True)]
    pallas_call x0 -> x1, Pallas kernels: none -> 104 us  [per_device_fused(): pl.pallas_call(functools.partial(kernel, tiles, tm_size), out_shape=jax.S...]
    ppermute x3 -> x0, waiting for transfers between devices: 30.3 us -> none  [shifted_2(): return lax.ppermute(block, axis, route)]
    gather x6 -> x0, local copies, waits for them, and re-layouts: 29.7 us -> none  [the longest x3 14.8 us: per_device(): lower_values = jnp.take(gathered, lower_source, axis=0)]
    select_n x40 -> x0, other arithmetic: 18.1 us -> none  [the longest x27 13.9 us: delay_columns(): jnp.where((shifts >> bit_index & 1)[:, None] == 1, shifted, extended)]
    unnamed x2, local copies, waits for them, and re-layouts: 0.01 us -> 4.78 us
    slice x16 -> x0, local copies, waits for them, and re-layouts: 4.36 us -> none  [the longest x9 0.96 us: delay_columns(): extended[:, :-stride]]
    ppermute x3 -> x0, starting transfers between devices: 4.28 us -> none  [shifted_2(): return lax.ppermute(block, axis, route)]
  transfers between devices with their start and end apart: 6 -> 0, of which waited for: 6 -> 0; matrix products, arithmetic and copies ran while one was open for 6% -> 0% of each run, Pallas kernels for 0% -> 0%
where the time goes in v1:
time: 109 us; the launch traced here: 108 us
  Pallas kernels  104 us (95%)
  local copies, waits for them, and re-layouts  4.78 us (4%)
    pallas_call x1, Pallas kernels, per_device_fused(): pl.pallas_call(functools.partial(kernel, tiles, tm_size), out_shape=jax.S...  104 us
    unnamed x2, local copies, waits for them, and re-layouts  4.78 us

profile of v1, /device:TPU:7, one launch (start us, length us, event | category | flops | bytes accessed | tf_op | source)
XLA Modules:
  0.0 108.5 jit_solution(15142230325262544711)
XLA Ops:
  0.0 2.4 %copy.6 = f32[32,8,8,128]{3,2,1,0:T(8,128)} copy(f32[32,8,8,128]{3,1,2,0:T(8,128)} %bitcast.8) | data formatting | bytes 2097152
  2.4 103.7 %shard_map.55 = f32[256,8,128]{2,1,0:T(8,128)} custom-call(f32[256,8,128]{2,1,0:T(8,128)} %bitcast.7, s32[3,2048]{1,0:T(4,128)} %lower.1, s32[3,2048]{1,0:T(4,128)} %upper.1, s32[3,2048]{1,0:T(4,128)} %delays.1, s32[7]{0:T(128)} %counts.1), custom_call_target="tpu_custom_call" | custom-call | tf_op jit(solution)/shard_map/pallas_call | solution.py:295
  106.1 2.4 %copy.9 = f32[32,8,8,128]{3,1,2,0:T(8,128)} copy(f32[32,8,8,128]{3,2,1,0:T(8,128)} %bitcast.6) | data formatting | bytes 2097152

commit v2 on v1

--- a/solution.py
+++ b/solution.py
@@ -10,7 +10,9 @@
 DMAX = 2048
 ITERS = 3
 LANES = 128
-UNROLL = 8
+SUBLANES = 8
+UNROLL = 16
+CHUNKS_0 = 4
 CHUNKS_1 = 8
 CHUNKS_2 = 16
 
@@ -81,7 +83,7 @@
         )
 
 
-def kernel(tiles, tm_size, x_ref, lower, upper, delays, counts, out_ref, b0, b1, b2, s0, s1, s2, local_sem):
+def kernel(tiles, tm_size, x_ref, lower, upper, delays, counts, out_ref, b0, b1, b2, final, s0, s1, s2):
     f, t = lax.axis_index("freq"), lax.axis_index("tm")
     c, z = lax.rem(f, 2), lax.div(f, 2)
     zb, half = lax.rem(z, 2), lax.div(z, 2)
@@ -144,17 +146,28 @@
         pl.when(cond)(action)
 
     rim0 = rows // LANES
-    own0 = Flow(b0, s0, 0, rows)
-    rim_out0 = Flow(b0, s0, 1, rows)
-    rim_in0 = Flow(b0, s0, 2, rows)
-    stage = pltpu.make_async_copy(x_ref, b0.at[pl.ds(c * rows, rows), pl.ds(tiles, tiles)], local_sem.at[0])
-    stage.start()
-    stage.wait()
-    own0.copy(0, c * rows, partner, tiles, tiles, tiles).start()
+    n0, chunk0 = CHUNKS_0, rows // CHUNKS_0
+    own0, rim_out0, rim_in0 = [Flow(b0, s0, kind * n0, chunk0) for kind in range(3)]
     upper0 = rows
-    send_rim0 = rim_out0.copy(0, upper0, later, 2 * tiles - rim0, tiles - rim0, rim0)
-    pass_rim0 = rim_in0.copy(0, upper0, partner, tiles - rim0, tiles - rim0, rim0)
-    when((c == 1) & has_later, send_rim0.start)
+    tail0 = (2 * tiles - rim0, tiles - rim0, rim0)
+    kept0 = (tiles - rim0, tiles - rim0, rim0)
+    full0 = (tiles, tiles, tiles)
+
+    def spread(first, count):
+        def body(step, carry):
+            r = first + step * SUBLANES
+            for tile in range(tiles):
+                b0[pl.ds(c * rows + r, SUBLANES), tiles + tile, :] = x_ref[
+                    pl.ds(r, SUBLANES), pl.ds(tile * LANES, LANES)
+                ]
+            return carry
+
+        lax.fori_loop(0, count // SUBLANES, body, 0)
+
+    for j in range(n0):
+        spread(j * chunk0, chunk0)
+        when((c == 1) & has_later, rim_out0.copy(j, upper0, later, *tail0).start)
+        own0.copy(j, c * rows, partner, *full0).start()
 
     @pl.when(t == 0)
     def _():
@@ -168,13 +181,16 @@
 
             lax.fori_loop(0, first // UNROLL, clear, 0)
 
-    @pl.when((c == 1) & has_earlier)
-    def _():
-        send_rim0.wait_recv()
-        pass_rim0.start()
-
-    own0.copy(0, (1 - c) * rows, partner, tiles, tiles, tiles).wait_recv()
-    when((c == 0) & has_earlier, pass_rim0.wait_recv)
+    for j in range(n0):
+
+        @pl.when((c == 1) & has_earlier)
+        def _():
+            rim_out0.copy(j, upper0, later, *tail0).wait_recv()
+            rim_in0.copy(j, upper0, partner, *kept0).start()
+
+    for j in range(n0):
+        own0.copy(j, (1 - c) * rows, partner, *full0).wait_recv()
+        when((c == 0) & has_earlier, rim_in0.copy(j, upper0, partner, *kept0).wait_recv)
 
     rim1 = 2 * rows // LANES
     n1, chunk1 = CHUNKS_1, rows // CHUNKS_1
@@ -256,13 +272,22 @@
         when(has_earlier, rim_in2.copy(j, upper2 + across, partner, *kept2).wait_recv)
 
     def store_out(i, value):
-        out_ref[i] = value
+        final[i] = value
 
     merge(2, b2, f * rows, f * rows, 0, rows, store_out)
 
-    own0.copy(0, c * rows, partner, *wide).wait_send()
-    when((c == 1) & has_later, send_rim0.wait_send)
-    when((c == 1) & has_earlier, pass_rim0.wait_send)
+    def flatten(step, carry):
+        r = step * SUBLANES
+        for tile in range(tiles):
+            out_ref[pl.ds(r, SUBLANES), pl.ds(tile * LANES, LANES)] = final[pl.ds(r, SUBLANES), tile, :]
+        return carry
+
+    lax.fori_loop(0, rows // SUBLANES, flatten, 0)
+
+    for j in range(n0):
+        own0.copy(j, c * rows, partner, *full0).wait_send()
+        when((c == 1) & has_later, rim_out0.copy(j, upper0, later, *tail0).wait_send)
+        when((c == 1) & has_earlier, rim_in0.copy(j, upper0, partner, *kept0).wait_send)
     for j in range(n1):
         pair1.copy(j, mine1, pair, *wide).wait_send()
         own1.copy(j, mine1, partner, *wide).wait_send()
@@ -292,25 +317,24 @@
     row_count, samples = band_state.shape
     tiles = samples // LANES
     dma = pltpu.SemaphoreType.DMA
-    out = pl.pallas_call(
+    return pl.pallas_call(
         functools.partial(kernel, tiles, tm_size),
-        out_shape=jax.ShapeDtypeStruct((row_count, tiles, LANES), jnp.float32),
+        out_shape=jax.ShapeDtypeStruct((row_count, samples), jnp.float32),
         in_specs=[pl.BlockSpec(memory_space=pltpu.VMEM)] + [pl.BlockSpec(memory_space=pltpu.SMEM)] * 4,
         out_specs=pl.BlockSpec(memory_space=pltpu.VMEM),
         scratch_shapes=[
             pltpu.VMEM((2 * row_count, 2 * tiles, LANES), jnp.float32),
             pltpu.VMEM((4 * row_count, 2 * tiles, LANES), jnp.float32),
             pltpu.VMEM((8 * row_count, 2 * tiles, LANES), jnp.float32),
-            dma((2, 3)),
+            pltpu.VMEM((row_count, tiles, LANES), jnp.float32),
+            dma((2, 3 * CHUNKS_0)),
             dma((2, 5 * CHUNKS_1)),
             dma((2, 6 * CHUNKS_2)),
-            dma((1,)),
         ],
         compiler_params=pltpu.CompilerParams(
             collective_id=0, has_side_effects=True, vmem_limit_bytes=60 * 2**20
         ),
-    )(band_state.reshape(row_count, tiles, LANES), lower_rows, upper_rows, delays, counts)
-    return out.reshape(row_count, samples)
+    )(band_state, lower_rows, upper_rows, delays, counts)
 
 
 def solution(mesh):

time: 109 us -> 106 us (0.972)
  local copies, waits for them, and re-layouts: 4.78 us -> 2.31 us
    unnamed x2 -> x1, local copies, waits for them, and re-layouts: 4.78 us -> 2.31 us
where the time goes in v2:
time: 106 us
  Pallas kernels  103 us (97%)
  local copies, waits for them, and re-layouts  2.31 us (2%)
    pallas_call x1, Pallas kernels, per_device_fused(): pl.pallas_call(functools.partial(kernel, tiles, tm_size), out_shape=jax.S...  103 us
    unnamed x1, local copies, waits for them, and re-layouts  2.31 us

profile of v2, /device:TPU:7, one launch (start us, length us, event | category | flops | bytes accessed | tf_op | source)
XLA Modules:
  0.0 105.8 jit_solution(8646621816564815206)
XLA Ops:
  0.0 103.4 %shard_map.55 = f32[256,1024]{1,0:T(8,128)} custom-call(f32[256,1024]{1,0:T(8,128)} %x_ref.1, s32[3,2048]{1,0:T(4,128)} %lower.1, s32[3,2048]{1,0:T(4,128)} %upper.1, s32[3,2048]{1,0:T(4,128)} %delays.1, s32[7]{0:T(128)} %counts.1), custom_call_target="tpu_custom_call" | custom-call | tf_op jit(solution)/shard_map/pallas_call | solution.py:320
  103.5 2.3 %copy.7 = f32[256,1024]{1,0:T(8,128)} copy(f32[256,1024]{1,0:T(8,128)} %shard_map.55) | data formatting | bytes 2097152
